TPU v7x, 32 devices: a whole 2x2x4 slice. The times are simulated.
32 devices in a mesh: rep: 2 (over x), dp: 16 (over y, z, core).
Axes of the slice: x: 2, y: 2, z: 4, core: 2. Of those that a mesh axis runs over, the one named last changes fastest.
Arguments:
- g_w_gate: bfloat16 [32, 2, 1024, 3200], P(('rep', 'dp')), parts along dimension 0
- g_w_up: bfloat16 [32, 2, 1024, 3200], P(('rep', 'dp')), parts along dimension 0
- g_w_down: bfloat16 [32, 2, 3200, 1024], P(('rep', 'dp')), parts along dimension 0
- w_gate: bfloat16 [2, 1024, 3200], replicated
- w_up: bfloat16 [2, 1024, 3200], replicated
- w_down: bfloat16 [2, 3200, 1024], replicated
- m_w_gate: float32 [2, 1024, 3200], P(None, 'dp')
- m_w_up: float32 [2, 1024, 3200], P(None, 'dp')
- m_w_down: float32 [2, 3200, 1024], P(None, 'dp')
- v_w_gate: float32 [2, 1024, 3200], P(None, 'dp')
- v_w_up: float32 [2, 1024, 3200], P(None, 'dp')
- v_w_down: float32 [2, 3200, 1024], P(None, 'dp')
Outputs:
- output 1: bfloat16 [4, 1024, 3200], P('rep'), parts along dimension 0
- output 2: bfloat16 [4, 1024, 3200], P('rep'), parts along dimension 0
- output 3: bfloat16 [4, 3200, 1024], P('rep'), parts along dimension 0
- output 4: float32 [4, 1024, 3200], P('rep', 'dp'), parts along dimension 0
- output 5: float32 [4, 1024, 3200], P('rep', 'dp'), parts along dimension 0
- output 6: float32 [4, 3200, 1024], P('rep', 'dp'), parts along dimension 0
- output 7: float32 [4, 1024, 3200], P('rep', 'dp'), parts along dimension 0
- output 8: float32 [4, 1024, 3200], P('rep', 'dp'), parts along dimension 0
- output 9: float32 [4, 3200, 1024], P('rep', 'dp'), parts along dimension 0
There are 2 independent parts. A program takes and returns all parts, laid end to end along the dimension named above; an argument that names none is the same for every part.
All inputs are finite; a program needn't handle non-finite values.
Results may differ from a plain program's by a relative error of at most 0.022.
Values are sent between devices in bfloat16 or wider.
A program may use at most 2 GiB of HBM per device.

v0:
```python
import jax
import jax.numpy as jnp
from jax import lax
from jax.sharding import PartitionSpec as P


def adamw(w, m, v, g):
    m = 0.9 * m + 0.1 * g
    v = 0.95 * v + 0.05 * g * g
    step = m * lax.rsqrt(v + 1e-8) + 0.1 * w
    return (w - 0.02 * step).astype(jnp.bfloat16), m, v


def solution(mesh):
    def step(*arrays):
        terms, weights, m, v = (arrays[i : i + 3] for i in (0, 3, 6, 9))
        gradients = [lax.psum_scatter(t[0], "dp", scatter_dimension=1, tiled=True).astype(jnp.float32) for t in terms]
        me = lax.axis_index("dp")
        own = [lax.dynamic_slice_in_dim(w, me * one.shape[1], one.shape[1], 1).astype(jnp.float32) for w, one in zip(weights, m, strict=True)]
        new = [adamw(w, m, v, g) for w, m, v, g in zip(own, m, v, gradients, strict=True)]
        whole = [lax.all_gather(one[0], "dp", axis=1, tiled=True) for one in new]
        return (*whole, *(one[1] for one in new), *(one[2] for one in new))

    all_of, cut = P(None, None, None), P(None, "dp", None)
    return jax.shard_map(
        step,
        mesh=mesh,
        in_specs=(P(("rep", "dp"), None, None, None),) * 3 + (all_of,) * 3 + (cut,) * 6,
        out_specs=(P("rep", None, None),) * 3 + (P("rep", "dp", None),) * 6,
        check_vma=False,
    )
```

profile of v0, /device:TPU:0, one launch (start us, length us, event | category | flops | bytes accessed | tf_op | source)
XLA Modules:
  0.0 782.0 jit_solution(9415327432404060874)
XLA Ops:
  7.2 0.0 reduce-scatter.8.cloned.1.call-start
  7.2 0.7 reduce-scatter.8.cloned.1.call-update
  7.9 0.0 reduce-scatter.6.cloned.1.call-start
  8.0 0.7 reduce-scatter.6.cloned.1.call-update
  8.7 0.0 reduce-scatter.10.cloned.1.call-start
  8.7 22.1 %copy.21 = bf16[2,3200,1024]{2,0,1:T(2,128)(2,1)S(1)} copy(bf16[2,3200,1024]{2,1,0:T(8,128)(2,1)} %bitcast.9) | data formatting | bytes 26214400
  30.8 7.4 copy.23
  38.2 0.0 copy-start.1
  38.2 0.0 copy-start.2
  38.2 0.0 reduce-scatter.10.cloned.1.call-update
  38.2 0.0 all-gather.6.cloned.1.call-start
  38.3 113.6 %reduce-scatter.8.cloned.1.call-done = bf16[2,64,3200]{2,1,0:T(8,128)(2,1)} async-done(((bf16[2,1024,3200]{2,1,0:T(8,128)(2,1)}), bf16[2,64,3200]{2,1,0:T(8,128)(2,1)}) %reduce-scatter.8.cloned.1.call-update) | async-done | bytes 819216 | tf_op jit(solution)/shard_map/reduce_scatter | solution.py:17
  151.9 0.0 copy-done.1
  151.9 0.0 copy-done.2
  151.9 3.8 fusion.6
  155.6 0.0 all-gather.6.cloned.1.call-update
  155.7 0.0 all-gather.4.cloned.1.call-start
  155.7 136.9 %reduce-scatter.6.cloned.1.call-done = bf16[2,64,3200]{2,1,0:T(8,128)(2,1)} async-done(((bf16[2,1024,3200]{2,1,0:T(8,128)(2,1)}), bf16[2,64,3200]{2,1,0:T(8,128)(2,1)}) %reduce-scatter.6.cloned.1.call-update) | async-done | bytes 819216 | tf_op jit(solution)/shard_map/reduce_scatter | solution.py:17
  292.6 4.8 fusion.2
  297.4 0.0 copy-start.3
  297.4 0.0 all-gather.4.cloned.1.call-update
  297.4 0.0 all-gather.8.cloned.1.call-start
  297.5 136.4 %reduce-scatter.10.cloned.1.call-done = bf16[200,2048]{1,0:T(8,128)(2,1)} async-done(((bf16[3200,2048]{1,0:T(8,128)(2,1)}), bf16[200,2048]{1,0:T(8,128)(2,1)}) %reduce-scatter.10.cloned.1.call-update) | async-done | bytes 819216
  433.9 2.6 reshape.19
  436.5 0.0 copy-done.3
  436.5 4.2 fusion.10
  440.8 0.0 all-gather.8.cloned.1.call-update
  440.8 98.7 %all-gather.6.cloned.1.call-done = bf16[2,1024,3200]{2,1,0:T(8,128)(2,1)} async-done(((bf16[2,64,3200]{2,1,0:T(8,128)(2,1)}), bf16[2,1024,3200]{2,1,0:T(8,128)(2,1)}) %all-gather.6.cloned.1.call-update) | async-done | bytes 13107216 | tf_op jit(solution)/shard_map/all_gather | solution.py:21
  539.5 104.4 %all-gather.4.cloned.1.call-done = bf16[2,1024,3200]{2,1,0:T(8,128)(2,1)} async-done(((bf16[2,64,3200]{2,1,0:T(8,128)(2,1)}), bf16[2,1024,3200]{2,1,0:T(8,128)(2,1)}) %all-gather.4.cloned.1.call-update) | async-done | bytes 13107216 | tf_op jit(solution)/shard_map/all_gather | solution.py:21
  644.0 104.4 %all-gather.8.cloned.1.call-done = bf16[2,3200,1024]{2,1,0:T(8,128)(2,1)} async-done(((bf16[2,200,1024]{2,1,0:T(8,128)(2,1)}), bf16[2,3200,1024]{2,1,0:T(8,128)(2,1)}) %all-gather.8.cloned.1.call-update) | async-done | bytes 13107216 | tf_op jit(solution)/shard_map/all_gather | solution.py:21
  748.4 0.0 copy-start
  748.4 0.0 slice-start
  748.4 0.0 slice-start.1
  748.4 12.7 %copy.31 = bf16[2,1024,3200]{2,1,0:T(8,128)(2,1)} copy(bf16[2,1024,3200]{2,1,0:T(8,128)(2,1)} %all-gather.4.cloned.1.call-done) | data formatting | bytes 26214400
  761.1 0.0 copy-done
  761.1 0.0 slice-start.2
  761.1 0.0 slice-start.3
  761.1 6.6 copy.32
  767.7 0.0 slice-done
  767.8 1.2 slice-done.1
  768.9 1.3 slice-done.2
  770.2 0.0 slice-done.3
  770.2 4.9 copy.33
  (1 shorter events, 0.0 us)
Async XLA Ops:
  7.2 144.7 %reduce-scatter.8.cloned.1.call-start = ((), (), s32[]{:S(2)}) async-start(), calls=%async_computation.5 | async-start | bytes 13926400 | tf_op jit(solution)/shard_map/reduce_scatter | solution.py:17
  7.9 284.7 %reduce-scatter.6.cloned.1.call-start = ((), (), s32[]{:S(2)}) async-start(), calls=%async_computation.3 | async-start | bytes 13926400 | tf_op jit(solution)/shard_map/reduce_scatter | solution.py:17
  8.7 425.2 %reduce-scatter.10.cloned.1.call-start = ((), (), s32[]{:S(2)}) async-start(), calls=%async_computation.8 | async-start | bytes 13926400
  38.2 113.7 %copy-start.1 = (f32[2,64,3200]{2,1,0:T(8,128)S(1)}, f32[2,64,3200]{2,1,0:T(8,128)}, u32[]{:S(2)}) copy-start(f32[2,64,3200]{2,1,0:T(8,128)} %param.22) | copy-start | bytes 4915204
  38.2 113.7 %copy-start.2 = (f32[2,64,3200]{2,1,0:T(8,128)S(1)}, f32[2,64,3200]{2,1,0:T(8,128)}, u32[]{:S(2)}) copy-start(f32[2,64,3200]{2,1,0:T(8,128)} %param.19) | copy-start | bytes 4915204
  38.2 501.3 %all-gather.6.cloned.1.call-start = ((), (), s32[]{:S(2)}) async-start(), calls=%async_computation.6 | async-start | bytes 13926400 | tf_op jit(solution)/shard_map/all_gather | solution.py:21
  155.7 488.3 %all-gather.4.cloned.1.call-start = ((), (), s32[]{:S(2)}) async-start(), calls=%async_computation.4 | async-start | bytes 13926400 | tf_op jit(solution)/shard_map/all_gather | solution.py:21
  297.4 139.1 %copy-start.3 = (f32[2,200,1024]{2,1,0:T(8,128)S(1)}, f32[2,200,1024]{2,1,0:T(8,128)}, u32[]{:S(2)}) copy-start(f32[2,200,1024]{2,1,0:T(8,128)} %param.23) | copy-start | bytes 4915204
  297.4 451.0 %all-gather.8.cloned.1.call-start = ((), (), s32[]{:S(2)}) async-start(), calls=%async_computation.7 | async-start | bytes 13926400 | tf_op jit(solution)/shard_map/all_gather | solution.py:21
  748.4 12.7 %copy-start = (bf16[2,1024,3200]{2,1,0:T(8,128)(2,1)S(1)}, bf16[2,1024,3200]{2,1,0:T(8,128)(2,1)}, u32[]{:S(2)}) copy-start(bf16[2,1024,3200]{2,1,0:T(8,128)(2,1)} %all-gather.6.cloned.1.call-done) | copy-start | bytes 39321604
  748.4 19.4 %slice-start = ((s8[13107200]{0:T(1024)(128)(4,1)}), s8[4194304]{0:T(1024)(128)(4,1)S(1)}, s32[]{:S(2)}) async-start(s8[13107200]{0:T(1024)(128)(4,1)} %bitcast.12), calls=%async_computation.9 | async-start | bytes 8388608
  748.4 20.5 %slice-start.1 = ((s8[13107200]{0:T(1024)(128)(4,1)}), s8[4194304]{0:T(1024)(128)(4,1)S(1)}, s32[]{:S(2)}) async-start(s8[13107200]{0:T(1024)(128)(4,1)} %bitcast.12), calls=%async_computation.10 | async-start | bytes 8388608
  761.1 9.1 %slice-start.2 = ((s8[13107200]{0:T(1024)(128)(4,1)}), s8[4194304]{0:T(1024)(128)(4,1)S(1)}, s32[]{:S(2)}) async-start(s8[13107200]{0:T(1024)(128)(4,1)} %bitcast.12), calls=%async_computation.11 | async-start | bytes 8388608
  761.1 9.1 %slice-start.3 = ((s8[13107200]{0:T(1024)(128)(4,1)}), s8[524288]{0:T(1024)(128)(4,1)S(1)}, s32[]{:S(2)}) async-start(s8[13107200]{0:T(1024)(128)(4,1)} %bitcast.12), calls=%async_computation.12 | async-start | bytes 1048576
Sparse Core Ops, SparseCore 0:
  12.1 139.7 reduce-scatter.7
  155.9 136.6 reduce-scatter.5
  297.3 136.5 reduce-scatter.9
  436.6 102.9 all-gather.5
  542.2 101.7 all-gather.3
  646.6 101.7 all-gather.7
where the time goes:
time: 782 us
  waiting for transfers between devices  696 us (89%)
  local copies, waits for them, and re-layouts  58.8 us (8%)
  between operations  14.2 us (2%)
  other arithmetic  12.8 us (2%)
    all_gather x3, waiting for transfers between devices, step(): whole = [lax.all_gather(one[0], 'dp', axis=1, tiled=True) for one in new]  308 us
    reduce_scatter x2, waiting for transfers between devices, step(): lax.psum_scatter(t[0], 'dp', scatter_dimension=1, tiled=True)  250 us
    unnamed x7, waiting for transfers between devices  138 us
    unnamed x22, local copies, waits for them, and re-layouts  58.8 us
  transfers between devices with their start and end apart: 6, of which 6 were waited for; matrix products, arithmetic and copies ran while one was open for 6% of the time, Pallas kernels for 0%

commit v1 on v0

v1 whole, which is shorter than its diff:
```python
import functools

import jax
import jax.numpy as jnp
from jax import lax
from jax.experimental import pallas as pl
from jax.experimental.pallas import tpu as pltpu
from jax.sharding import PartitionSpec as P

PIECES = 10
RING = 8
LAG = 4
F32, BF16 = jnp.float32, jnp.bfloat16


def kernel(pieces, tiles, near, refs_in, refs_out, scratch):
    g_in, w_in, m_in, v_in = (refs_in[i : i + 3] for i in (0, 3, 6, 9))
    out, m_out, v_out = refs_out
    (G, CL, A1, AL, AR, BL, BR, B2, NW, W, M, V, GS) = scratch[:13]
    (l_g, l_mv, l_st, l_out) = scratch[13:17]
    (r_core, r_a1, r_al, r_ar, r_bl, r_br, r_b2, r_yo, r_az, r_ay, r_bz, r_co) = scratch[17:29]
    (s_core, s_a1, s_al, s_ar, s_bl, s_br, s_b2, s_yo, s_azr, s_azl, s_ay, s_bzr, s_bzl, s_co) = scratch[29:]
    T = tiles // pieces
    TA, TB = near, T - near
    N = 6 * pieces
    x, me = lax.axis_index("rep"), lax.axis_index("dp")
    core, z, y = me % 2, (me // 2) % 4, me // 8
    partner, right, left, across = me + 1 - 2 * core, me + 2, me - 2, me + 8 - 16 * y

    barrier = pltpu.get_barrier_semaphore()

    def greet(device):
        pl.semaphore_signal(barrier, inc=1, device_id=(x, device), device_id_type=pl.DeviceIdType.MESH)

    greet(partner)
    greet(across)

    @pl.when(z > 0)
    def _():
        greet(left)

    @pl.when(z < 3)
    def _():
        greet(right)

    pl.semaphore_wait(barrier, 2 + jnp.where(z > 0, 1, 0) + jnp.where(z < 3, 1, 0))

    def copy(src, dst, ss, rs, device):
        return pltpu.make_async_remote_copy(
            src_ref=src, dst_ref=dst, send_sem=ss, recv_sem=rs, device_id=(x, device), device_id_type=pl.DeviceIdType.MESH
        )

    def place(c):
        w = c // (2 * pieces)
        r = c - w * 2 * pieces
        layer = r // pieces
        return w, layer, (r - layer * pieces) * T

    both, row, near_part, far_part = pl.ds(0, 2), pl.ds(0, 4), pl.ds(0, TA), pl.ds(TA, TB)

    def c_core(c, i):
        _, layer, at = place(c)
        src = g_in[i].at[layer, both, row, 1 - core, pl.ds(at, T)]
        return copy(src, CL.at[c], s_core.at[c % RING], r_core.at[c], partner)

    def c_g(c, i):
        _, layer, at = place(c)
        return pltpu.make_async_copy(g_in[i].at[layer, both, row, core, pl.ds(at, T)], G.at[c % RING], l_g.at[c % RING])

    def c_load(c, i):
        _, layer, at = place(c)
        k = c % 4
        return (
            pltpu.make_async_copy(m_in[i].at[layer, pl.ds(at, T)], M.at[k], l_mv.at[k, 0]),
            pltpu.make_async_copy(v_in[i].at[layer, pl.ds(at, T)], V.at[k], l_mv.at[k, 1]),
            pltpu.make_async_copy(w_in[i].at[layer, y, z, core, pl.ds(at, T)], W.at[k], l_mv.at[k, 2]),
        )

    def c_store(c):
        w, layer, at = place(c)
        k = c % 4
        return (
            pltpu.make_async_copy(M.at[k], m_out.at[w, layer, pl.ds(at, T)], l_st.at[k, 0]),
            pltpu.make_async_copy(V.at[k], v_out.at[w, layer, pl.ds(at, T)], l_st.at[k, 1]),
        )

    def c_a1(c):
        return copy(CL.at[c, 1 - y, row, near_part], A1.at[c], s_a1.at[c % RING], r_a1.at[c], across)

    def c_a2(c, b, go_right):
        land, rs, ss, k, device = (AL, r_al, s_al, b - 1, right) if go_right else (AR, r_ar, s_ar, b, left)
        return copy(CL.at[c, y, b, near_part], land.at[c, k], ss.at[c % RING, k], rs.at[c, k], device)

    def c_b1(c, b, go_right):
        land, rs, ss, k, device = (BL, r_bl, s_bl, b - 1, right) if go_right else (BR, r_br, s_br, b, left)
        return copy(CL.at[c, both, b, far_part], land.at[c, k], ss.at[c % RING, k], rs.at[c, k], device)

    def c_b2(c):
        return copy(CL.at[c, 1 - y, z, far_part], B2.at[c], s_b2.at[c % RING], r_b2.at[c], across)

    def spot(c, rows, column, at, n):
        w, layer, start = place(c)
        return out.at[w, layer, rows, column, core, pl.ds(start + at, n)]

    def c_own(c):
        return pltpu.make_async_copy(NW.at[c % RING], spot(c, y, z, 0, T), l_out.at[c % RING])

    def c_yo(c):
        return copy(NW.at[c % RING], spot(c, y, z, 0, T), s_yo.at[c % RING], r_yo.at[c], across)

    def c_az(c, b, go_right, own=False):
        ss, device = (s_azr, right) if go_right else (s_azl, left)
        src = NW.at[c % RING, near_part] if own else spot(c, y, b, 0, TA)
        return copy(src, spot(c, y, b, 0, TA), ss.at[c % RING, b], r_az.at[c, b], device)

    def c_ay(c, b):
        return copy(spot(c, y, b, 0, TA), spot(c, y, b, 0, TA), s_ay.at[c % RING, b], r_ay.at[c, b], across)

    def c_bz(c, b, go_right):
        ss, device = (s_bzr, right) if go_right else (s_bzl, left)
        return copy(spot(c, both, b, TA, TB), spot(c, both, b, TA, TB), ss.at[c % RING, b], r_bz.at[c, b], device)

    def c_co(c, b):
        return copy(spot(c, both, b, 0, T), spot(c, both, b, 0, T), s_co.at[c % RING, b], r_co.at[c, b], partner)

    def start(copies):
        for one in copies if isinstance(copies, tuple) else (copies,):
            one.start()

    def sent(one):
        one.wait_send()

    def ok(c):
        return jnp.logical_and(c >= 0, c < N)

    def when(*conds):
        return pl.when(functools.reduce(jnp.logical_and, conds))

    def loop(low, high, body):
        lax.fori_loop(low, high, lambda i, _: (body(i), 0)[1], 0)

    def of_weight(c, do):
        w = c // (2 * pieces)
        for i in range(3):

            @pl.when(w == i)
            def _():
                do(i)

    def total(terms):
        return functools.reduce(jnp.add, (one.astype(F32) for one in terms))

    def a2(c, go_right, act, sums):
        def one(b):
            if sums:

                def put(inner):
                    terms = [G[c % RING, y, b, near_part], CL[c, y, b, near_part], A1[c, b]]
                    if inner:
                        terms.append(AL[c, b - 1] if go_right else AR[c, b])
                    CL[c, y, b, near_part] = total(terms).astype(BF16)

                pl.when(z == (0 if go_right else 3))(lambda: put(False))
                pl.when(z != (0 if go_right else 3))(lambda: put(True))
            act(c_a2(c, b, go_right))

        loop(z + 1, 4, one) if go_right else loop(0, z, one)

    def b1(c, go_right, act, sums):
        def one(b):
            if sums:

                def put(inner):
                    terms = [G[c % RING, both, b, far_part], CL[c, both, b, far_part]]
                    if inner:
                        terms.append(BL[c, b - 1] if go_right else BR[c, b])
                    CL[c, both, b, far_part] = total(terms).astype(BF16)

                pl.when(z == (0 if go_right else 3))(lambda: put(False))
                pl.when(z != (0 if go_right else 3))(lambda: put(True))
            act(c_b1(c, b, go_right))

        loop(z + 1, 4, one) if go_right else loop(0, z, one)

    def arrived(c, go_right, make):
        if go_right:
            when(z > 0)(lambda: loop(z, 4, lambda b: make(c, b, True).wait_recv()))
        else:
            when(z < 3)(lambda: loop(0, z + 1, lambda b: make(c, b, False).wait_recv()))

    def own_part(c, yy, part, with_rows, land_l, land_r, extra, put):
        def terms():
            return [G[c % RING, yy, z, part], CL[c, yy, z, part], *extra()]

        def from_left():
            return land_l[c, z - 1, yy] if with_rows else land_l[c, z - 1]

        def from_right():
            return land_r[c, z, yy] if with_rows else land_r[c, z]

        pl.when(z == 0)(lambda: put(total([*terms(), from_right()])))
        pl.when(z == 3)(lambda: put(total([*terms(), from_left()])))
        when(z > 0, z < 3)(lambda: put(total([*terms(), from_left(), from_right()])))

    def az(c, b, act, own=False):
        when(z < 3, b <= z)(lambda: act(c_az(c, b, True, own)))
        when(z > 0, b >= z)(lambda: act(c_az(c, b, False, own)))

    def bz(c, b, act):
        when(z < 3, b <= z)(lambda: act(c_bz(c, b, True)))
        when(z > 0, b >= z)(lambda: act(c_bz(c, b, False)))

    def step(t):
        @pl.when(t < N)
        def _():
            of_weight(t, lambda i: (start(c_core(t, i)), start(c_g(t, i))))

        c0 = t - 4

        @when(ok(c0))
        def _():
            @pl.when(c0 >= 4)
            def _():
                for one in c_store(c0 - 4):
                    one.wait()

            of_weight(c0, lambda i: start(c_load(c0, i)))

        tau = t - 2

        @when(ok(tau))
        def _():
            c_g(tau, 0).wait()
            c_core(tau, 0).wait_recv()

            def add(b):
                CL[tau, 1 - y, b, near_part] = total((G[tau % RING, 1 - y, b, near_part], CL[tau, 1 - y, b, near_part])).astype(BF16)

            loop(0, 4, add)
            c_a1(tau).start()

        for go_right in (True, False):
            c = tau - z if go_right else tau - 3 + z

            @when(ok(c))
            def _():
                arrived(c, go_right, c_b1)
                b1(c, go_right, start, True)

        @when(ok(tau - 1))
        def _():
            c_a1(tau - 1).wait_recv()

        for go_right in (True, False):
            c = tau - 1 - z if go_right else tau - 4 + z

            @when(ok(c))
            def _():
                arrived(c, go_right, c_a2)
                a2(c, go_right, start, True)

        c3 = tau - 3

        @when(ok(c3))
        def _():
            def put(value):
                CL[c3, 1 - y, z, far_part] = value.astype(BF16)

            own_part(c3, 1 - y, far_part, True, BL, BR, lambda: (), put)
            c_b2(c3).start()

        c4 = tau - 4

        @when(ok(c4))
        def _():
            c_b2(c4).wait_recv()
            for one in c_load(c4, 0):
                one.wait()

            def put_near(value):
                GS[near_part] = value.astype(BF16)

            def put_far(value):
                GS[far_part] = value.astype(BF16)

            own_part(c4, y, near_part, False, AL, AR, lambda: (A1[c4, z],), put_near)
            own_part(c4, y, far_part, True, BL, BR, lambda: (B2[c4],), put_far)
            k = c4 % 4
            g = GS[...].astype(F32)
            m = 0.9 * M[k] + 0.1 * g
            v = 0.95 * V[k] + 0.05 * g * g
            w = W[k].astype(F32)
            NW[c4 % RING] = (w - 0.02 * (m * lax.rsqrt(v + 1e-8) + 0.1 * w)).astype(BF16)
            M[k] = m
            V[k] = v
            c_yo(c4).start()
            az(c4, z, start, True)
            c_own(c4).start()
            start(c_store(c4))

        for k in (1, 2, 3):
            c = tau - 4 - k
            for b, there in ((z - k, z - k >= 0), (z + k, z + k <= 3)):

                @when(ok(c), there)
                def _():
                    c_az(c, b, True).wait_recv()
                    az(c, b, start)
                    c_ay(c, b).start()

        for k in (0, 1, 2, 3):
            c = tau - 5 - k
            for b, there in ((z - k, z - k >= 0), (z + k, z + k <= 3))[: 1 if k == 0 else 2]:

                @when(ok(c), there)
                def _():
                    if k == 0:
                        c_yo(c).wait_recv()
                        c_own(c).wait()
                    else:
                        c_bz(c, b, True).wait_recv()
                        c_ay(c, b).wait_recv()
                    bz(c, b, start)
                    c_co(c, b).start()

        c10 = tau - 10

        @when(ok(c10))
        def _():
            loop(0, 4, lambda b: c_co(c10, b).wait_recv())

        late = tau - LAG

        @when(ok(late + 2))
        def _():
            sent(c_core(late + 2, 0))

        @when(ok(late))
        def _():
            sent(c_a1(late))

        for go_right in (True, False):
            cb = late - z if go_right else late - 3 + z
            ca = late - 1 - z if go_right else late - 4 + z
            when(ok(cb))(lambda: b1(cb, go_right, sent, False))
            when(ok(ca))(lambda: a2(ca, go_right, sent, False))

        @when(ok(late - 3))
        def _():
            sent(c_b2(late - 3))

        @when(ok(late - 4))
        def _():
            sent(c_yo(late - 4))
            az(late - 4, z, sent, True)

        for k in (1, 2, 3):
            c = late - 4 - k
            for b, there in ((z - k, z - k >= 0), (z + k, z + k <= 3)):

                @when(ok(c), there)
                def _():
                    az(c, b, sent)
                    sent(c_ay(c, b))

        for k in (0, 1, 2, 3):
            c = late - 5 - k
            for b, there in ((z - k, z - k >= 0), (z + k, z + k <= 3))[: 1 if k == 0 else 2]:

                @when(ok(c), there)
                def _():
                    bz(c, b, sent)
                    sent(c_co(c, b))

    loop(0, N + 2 + 8 + LAG, step)
    for c in range(N - 4, N):
        for one in c_store(c):
            one.wait()


def whole_step(pieces, near, arrays):
    tiles = arrays[6].shape[1]
    T, N = tiles // pieces, 6 * pieces
    TA, TB = near, T - near
    tile = (16, 128)
    dma = pltpu.SemaphoreType.DMA
    scratch = [
        pltpu.VMEM((RING, 2, 4, T, *tile), BF16),
        pltpu.VMEM((N, 2, 4, T, *tile), BF16),
        pltpu.VMEM((N, 4, TA, *tile), BF16),
        pltpu.VMEM((N, 3, TA, *tile), BF16),
        pltpu.VMEM((N, 3, TA, *tile), BF16),
        pltpu.VMEM((N, 3, 2, TB, *tile), BF16),
        pltpu.VMEM((N, 3, 2, TB, *tile), BF16),
        pltpu.VMEM((N, TB, *tile), BF16),
        pltpu.VMEM((RING, T, *tile), BF16),
        pltpu.VMEM((4, T, *tile), BF16),
        pltpu.VMEM((4, T, *tile), F32),
        pltpu.VMEM((4, T, *tile), F32),
        pltpu.VMEM((T, *tile), BF16),
        dma((RING,)), dma((4, 3)), dma((4, 2)), dma((RING,)),
        dma((N,)), dma((N,)), dma((N, 3)), dma((N, 3)), dma((N, 3)), dma((N, 3)), dma((N,)), dma((N,)),
        dma((N, 4)), dma((N, 4)), dma((N, 4)), dma((N, 4)),
        dma((RING,)), dma((RING,)), dma((RING, 3)), dma((RING, 3)), dma((RING, 3)), dma((RING, 3)), dma((RING,)), dma((RING,)),
        dma((RING, 4)), dma((RING, 4)), dma((RING, 4)), dma((RING, 4)), dma((RING, 4)), dma((RING, 4)),
    ]

    def body(*refs):
        kernel(pieces, tiles, near, refs[:12], refs[12:15], refs[15:])

    hbm = pl.BlockSpec(memory_space=pl.ANY)
    return pl.pallas_call(
        body,
        out_shape=(
            jax.ShapeDtypeStruct((3, 2, 2, 4, 2, tiles, *tile), BF16),
            jax.ShapeDtypeStruct((3, 2, tiles, *tile), F32),
            jax.ShapeDtypeStruct((3, 2, tiles, *tile), F32),
        ),
        in_specs=[hbm] * 12,
        out_specs=(hbm,) * 3,
        scratch_shapes=scratch,
        compiler_params=pltpu.CompilerParams(collective_id=0, has_side_effects=True, vmem_limit_bytes=63 << 20),
    )(*arrays)


def to_tiles(a):
    _, r, c = a.shape
    return a.reshape(2, r // 8, 8, c // 128, 128).swapaxes(2, 3).reshape(2, -1, 16, 128)


def from_tiles(a, shape):
    _, r, c = shape
    return a.reshape(2, r // 8, c // 128, 8, 128).swapaxes(2, 3).reshape(shape)


def solution(mesh):
    def step(*arrays):
        arrays = [a.reshape(a.shape[-3:]) for a in arrays]
        tiled = [to_tiles(a) for a in arrays]
        blocks = tiled[6].shape[1]
        tiled = [t.reshape(2, 2, 4, 2, blocks, 16, 128) for t in tiled[:6]] + tiled[6:]
        w, m, v = whole_step(PIECES, 6 * blocks // (10 * PIECES), tiled)
        shapes, own = [a.shape for a in arrays[3:6]], [a.shape for a in arrays[6:9]]
        return (
            *(from_tiles(w[i], shapes[i]) for i in range(3)),
            *(from_tiles(m[i], own[i]) for i in range(3)),
            *(from_tiles(v[i], own[i]) for i in range(3)),
        )

    all_of, cut = P(None, None, None), P(None, "dp", None)
    return jax.shard_map(
        step,
        mesh=mesh,
        in_specs=(P(("rep", "dp"), None, None, None),) * 3 + (all_of,) * 3 + (cut,) * 6,
        out_specs=(P("rep", None, None),) * 3 + (P("rep", "dp", None),) * 6,
        check_vma=False,
    )
```

time: 782 us -> 377 us (0.48)
  waiting for transfers between devices: 696 us -> 0 us
  Pallas kernels: 0 us -> 343 us
  local copies, waits for them, and re-layouts: 58.8 us -> 33.1 us
  between operations: 14.2 us -> 0.66 us
  other arithmetic: 12.8 us -> 0 us
    pallas_call x0 -> x1, Pallas kernels: none -> 343 us  [whole_step(): pl.pallas_call(body, out_shape=(jax.ShapeDtypeStruct((3, 2, 2, 4, 2, tile...]
    all_gather x3 -> x0, waiting for transfers between devices: 308 us -> none  [step(): whole = [lax.all_gather(one[0], 'dp', axis=1, tiled=True) for one in new]]
    reduce_scatter x2 -> x0, waiting for transfers between devices: 250 us -> none  [step(): lax.psum_scatter(t[0], 'dp', scatter_dimension=1, tiled=True)]
    unnamed x7 -> x0, waiting for transfers between devices: 138 us -> none
    unnamed x22 -> x2, local copies, waits for them, and re-layouts: 58.8 us -> 0.01 us
    slice x0 -> x2, local copies, waits for them, and re-layouts: none -> 33.1 us  [the longest x1 26.8 us: step(): w[i]]
    convert_element_type x3 -> x0, other arithmetic: 12.8 us -> none  [adamw(): return ((w - 0.02 * step).astype(jnp.bfloat16), m, v)]
  transfers between devices with their start and end apart: 6 -> 0, of which waited for: 6 -> 0; matrix products, arithmetic and copies ran while one was open for 6% -> 0% of each run, Pallas kernels for 0% -> 0%
where the time goes in v1:
time: 377 us
  Pallas kernels  343 us (91%)
  local copies, waits for them, and re-layouts  33.1 us (9%)
    pallas_call x1, Pallas kernels, whole_step(): pl.pallas_call(body, out_shape=(jax.ShapeDtypeStruct((3, 2, 2, 4, 2, tile...  343 us
    slice x1, local copies, waits for them, and re-layouts, step(): w[i]  26.8 us

profile of v1, /device:TPU:0, one launch (start us, length us, event | category | flops | bytes accessed | tf_op | source)
XLA Modules:
  0.0 376.8 jit_solution(2161766322990884184)
XLA Ops:
  0.6 343.0 %shard_map.187 = (bf16[3,2,2,4,2,100,16,128]{7,6,5,4,3,2,1,0:T(8,128)(2,1)}, f32[3,2,100,16,128]{4,3,2,1,0:T(8,128)}, f32[3,2,100,16,128]{4,3,2,1,0:T(8,128)}) custom-call(bf16[2,2,4,2,100,16,128]{6,5,4,3,2,1,0:T(8,128)(2,1)} %bitcast.108, bf16[2,2,4,2,100,16,128]{6,5,4,3,2,1,0:T(8,128)(2,1)} %bitcast.109, bf16[2,2,4,2,100,16,128]{6,5,4,3,2,1,0:T(8,128)(2,1)} %bitcast.110, ...), custom_call_target="tpu_custom_call" | custom-call | tf_op jit(solution)/shard_map/pallas_call | solution.py:412
  343.7 0.0 copy-start
  343.7 26.8 %fusion = (bf16[1,2,2,4,2,100,16,128]{7,6,5,4,3,2,1,0:T(8,128)(2,1)}, bf16[1,2,2,4,2,100,16,128]{7,6,5,4,3,2,1,0:T(8,128)(2,1)}, bf16[1,2,2,4,2,100,16,128]{7,6,5,4,3,2,1,0:T(8,128)(2,1)}) fusion(bf16[3,2,2,4,2,100,16,128]{7,6,5,4,3,2,1,0:T(8,128)(2,1)} %get-tuple-element.12), kind=kLoop, calls=%fused_computation | loop fusion | bytes 78643200 | tf_op jit(solution)/shard_map/slice | solution.py:445
  370.5 0.0 copy-done
  370.5 6.3 %fusion.1 = (f32[1,2,100,16,128]{4,3,2,1,0:T(8,128)}, f32[1,2,100,16,128]{4,3,2,1,0:T(8,128)}, f32[1,2,100,16,128]{4,3,2,1,0:T(8,128)}, f32[1,2,100,16,128]{4,3,...) fusion(f32[3,2,100,16,128]{4,3,2,1,0:T(8,128)} %get-tuple-element.14, ...), kind=kLoop, calls=%fused_computation.1 | loop fusion | bytes 19660800 | tf_op jit(solution)/shard_map/slice | solution.py:447
Async XLA Ops:
  343.7 26.8 %copy-start = (f32[3,2,100,16,128]{4,3,2,1,0:T(8,128)S(1)}, f32[3,2,100,16,128]{4,3,2,1,0:T(8,128)}, u32[]{:S(2)}) copy-start(f32[3,2,100,16,128]{4,3,2,1,0:T(8,128)} %get-tuple-element.13) | copy-start | bytes 14745604

commit v2 on v1

v2 whole, which is shorter than its diff:
```python
import functools

import jax
import jax.numpy as jnp
from jax import lax
from jax.experimental import pallas as pl
from jax.experimental.pallas import tpu as pltpu
from jax.sharding import PartitionSpec as P

PIECES = 10
RING = 8
LAND = 16
LAG = 4
VMEM_LIMIT = 15 << 20
F32, BF16 = jnp.float32, jnp.bfloat16


def kernel(pieces, tiles, near, refs_in, refs_out, scratch):
    g_in, w_in, m_in, v_in = (refs_in[i : i + 3] for i in (0, 3, 6, 9))
    m_out, v_out, out = refs_out
    (G, CL, A1, AL, AR, BL, BR, B2, W, GS) = scratch[:10]
    (l_g, l_mv) = scratch[10:12]
    (r_core, r_a1, r_al, r_ar, r_bl, r_br, r_b2, r_yo, r_az, r_ay, r_bz, r_co) = scratch[12:24]
    (s_core, s_a1, s_al, s_ar, s_bl, s_br, s_b2, s_yo, s_azr, s_azl, s_ay, s_bzr, s_bzl, s_co) = scratch[24:]
    T = tiles // pieces
    TA, TB = near, T - near
    N = 6 * pieces
    x, me = lax.axis_index("rep"), lax.axis_index("dp")
    core, z, y = me % 2, (me // 2) % 4, me // 8
    partner, right, left, across = me + 1 - 2 * core, me + 2, me - 2, me + 8 - 16 * y

    barrier = pltpu.get_barrier_semaphore()

    def greet(device):
        pl.semaphore_signal(barrier, inc=1, device_id=(x, device), device_id_type=pl.DeviceIdType.MESH)

    greet(partner)
    greet(across)

    @pl.when(z > 0)
    def _():
        greet(left)

    @pl.when(z < 3)
    def _():
        greet(right)

    pl.semaphore_wait(barrier, 2 + jnp.where(z > 0, 1, 0) + jnp.where(z < 3, 1, 0))

    def copy(src, dst, ss, rs, device):
        return pltpu.make_async_remote_copy(
            src_ref=src, dst_ref=dst, send_sem=ss, recv_sem=rs, device_id=(x, device), device_id_type=pl.DeviceIdType.MESH
        )

    def place(c):
        w = c // (2 * pieces)
        r = c - w * 2 * pieces
        layer = r // pieces
        return w, layer, (r - layer * pieces) * T

    both, row, near_part, far_part = pl.ds(0, 2), pl.ds(0, 4), pl.ds(0, TA), pl.ds(TA, TB)

    def c_core(c, i):
        _, layer, at = place(c)
        src = g_in[i].at[layer, both, row, 1 - core, pl.ds(at, T)]
        return copy(src, CL.at[c % LAND], s_core.at[c % RING], r_core.at[c % LAND], partner)

    def c_g(c, i):
        _, layer, at = place(c)
        return pltpu.make_async_copy(g_in[i].at[layer, both, row, core, pl.ds(at, T)], G.at[c % RING], l_g.at[c % RING])

    def c_load(c, i):
        w, layer, at = place(c)
        k = c % 4
        return (
            pltpu.make_async_copy(m_in[i].at[layer, pl.ds(at, T)], m_out.at[w, layer, pl.ds(at, T)], l_mv.at[k, 0]),
            pltpu.make_async_copy(v_in[i].at[layer, pl.ds(at, T)], v_out.at[w, layer, pl.ds(at, T)], l_mv.at[k, 1]),
            pltpu.make_async_copy(w_in[i].at[layer, y, z, core, pl.ds(at, T)], W.at[k], l_mv.at[k, 2]),
        )

    def c_a1(c):
        return copy(CL.at[c % LAND, 1 - y, row, near_part], A1.at[c % LAND], s_a1.at[c % RING], r_a1.at[c % LAND], across)

    def c_a2(c, b, go_right):
        land, rs, ss, k, device = (AL, r_al, s_al, b - 1, right) if go_right else (AR, r_ar, s_ar, b, left)
        return copy(CL.at[c % LAND, y, b, near_part], land.at[c % LAND, k], ss.at[c % RING, k], rs.at[c % LAND, k], device)

    def c_b1(c, b, go_right):
        land, rs, ss, k, device = (BL, r_bl, s_bl, b - 1, right) if go_right else (BR, r_br, s_br, b, left)
        return copy(CL.at[c % LAND, both, b, far_part], land.at[c % LAND, k], ss.at[c % RING, k], rs.at[c % LAND, k], device)

    def c_b2(c):
        return copy(CL.at[c % LAND, 1 - y, z, far_part], B2.at[c % LAND], s_b2.at[c % RING], r_b2.at[c % LAND], across)

    def spot(c, rows, column, at, n):
        w, layer, start = place(c)
        return out.at[w, layer, rows, column, core, pl.ds(start + at, n)]

    def c_yo(c):
        return copy(spot(c, y, z, 0, T), spot(c, y, z, 0, T), s_yo.at[c % RING], r_yo.at[c % LAND], across)

    def c_az(c, b, go_right):
        ss, device = (s_azr, right) if go_right else (s_azl, left)
        return copy(spot(c, y, b, 0, TA), spot(c, y, b, 0, TA), ss.at[c % RING, b], r_az.at[c % LAND, b], device)

    def c_ay(c, b):
        return copy(spot(c, y, b, 0, TA), spot(c, y, b, 0, TA), s_ay.at[c % RING, b], r_ay.at[c % LAND, b], across)

    def c_bz(c, b, go_right):
        ss, device = (s_bzr, right) if go_right else (s_bzl, left)
        return copy(spot(c, both, b, TA, TB), spot(c, both, b, TA, TB), ss.at[c % RING, b], r_bz.at[c % LAND, b], device)

    def c_co(c, b):
        return copy(spot(c, both, b, 0, T), spot(c, both, b, 0, T), s_co.at[c % RING, b], r_co.at[c % LAND, b], partner)

    def start(copies):
        for one in copies if isinstance(copies, tuple) else (copies,):
            one.start()

    def sent(one):
        one.wait_send()

    def ok(c):
        return jnp.logical_and(c >= 0, c < N)

    def when(*conds):
        return pl.when(functools.reduce(jnp.logical_and, conds))

    def loop(low, high, body):
        lax.fori_loop(low, high, lambda i, _: (body(i), 0)[1], 0)

    def of_weight(c, do):
        w = c // (2 * pieces)
        for i in range(3):

            @pl.when(w == i)
            def _():
                do(i)

    def total(terms):
        return functools.reduce(jnp.add, (one.astype(F32) for one in terms))

    def a2(c, go_right, act, sums):
        def one(b):
            if sums:

                def put(inner):
                    terms = [G[c % RING, y, b, near_part], CL[c % LAND, y, b, near_part], A1[c % LAND, b]]
                    if inner:
                        terms.append(AL[c % LAND, b - 1] if go_right else AR[c % LAND, b])
                    CL[c % LAND, y, b, near_part] = total(terms).astype(BF16)

                pl.when(z == (0 if go_right else 3))(lambda: put(False))
                pl.when(z != (0 if go_right else 3))(lambda: put(True))
            act(c_a2(c, b, go_right))

        loop(z + 1, 4, one) if go_right else loop(0, z, one)

    def b1(c, go_right, act, sums):
        def one(b):
            if sums:

                def put(inner):
                    terms = [G[c % RING, both, b, far_part], CL[c % LAND, both, b, far_part]]
                    if inner:
                        terms.append(BL[c % LAND, b - 1] if go_right else BR[c % LAND, b])
                    CL[c % LAND, both, b, far_part] = total(terms).astype(BF16)

                pl.when(z == (0 if go_right else 3))(lambda: put(False))
                pl.when(z != (0 if go_right else 3))(lambda: put(True))
            act(c_b1(c, b, go_right))

        loop(z + 1, 4, one) if go_right else loop(0, z, one)

    def arrived(c, go_right, make):
        if go_right:
            when(z > 0)(lambda: loop(z, 4, lambda b: make(c, b, True).wait_recv()))
        else:
            when(z < 3)(lambda: loop(0, z + 1, lambda b: make(c, b, False).wait_recv()))

    def own_part(c, yy, part, with_rows, land_l, land_r, extra, put):
        def terms():
            return [G[c % RING, yy, z, part], CL[c % LAND, yy, z, part], *extra()]

        def from_left():
            return land_l[c % LAND, z - 1, yy] if with_rows else land_l[c % LAND, z - 1]

        def from_right():
            return land_r[c % LAND, z, yy] if with_rows else land_r[c % LAND, z]

        pl.when(z == 0)(lambda: put(total([*terms(), from_right()])))
        pl.when(z == 3)(lambda: put(total([*terms(), from_left()])))
        when(z > 0, z < 3)(lambda: put(total([*terms(), from_left(), from_right()])))

    def az(c, b, act):
        when(z < 3, b <= z)(lambda: act(c_az(c, b, True)))
        when(z > 0, b >= z)(lambda: act(c_az(c, b, False)))

    def bz(c, b, act):
        when(z < 3, b <= z)(lambda: act(c_bz(c, b, True)))
        when(z > 0, b >= z)(lambda: act(c_bz(c, b, False)))

    def step(t):
        @pl.when(t < N)
        def _():
            of_weight(t, lambda i: (start(c_core(t, i)), start(c_g(t, i))))

        c0 = t - 4

        @when(ok(c0))
        def _():
            of_weight(c0, lambda i: start(c_load(c0, i)))

        tau = t - 2

        @when(ok(tau))
        def _():
            c_g(tau, 0).wait()
            c_core(tau, 0).wait_recv()

            def add(b):
                CL[tau % LAND, 1 - y, b, near_part] = total((G[tau % RING, 1 - y, b, near_part], CL[tau % LAND, 1 - y, b, near_part])).astype(BF16)

            loop(0, 4, add)
            c_a1(tau).start()

        for go_right in (True, False):
            c = tau - z if go_right else tau - 3 + z

            @when(ok(c))
            def _():
                arrived(c, go_right, c_b1)
                b1(c, go_right, start, True)

        @when(ok(tau - 1))
        def _():
            c_a1(tau - 1).wait_recv()

        for go_right in (True, False):
            c = tau - 1 - z if go_right else tau - 4 + z

            @when(ok(c))
            def _():
                arrived(c, go_right, c_a2)
                a2(c, go_right, start, True)

        c3 = tau - 3

        @when(ok(c3))
        def _():
            def put(value):
                CL[c3 % LAND, 1 - y, z, far_part] = value.astype(BF16)

            own_part(c3, 1 - y, far_part, True, BL, BR, lambda: (), put)
            c_b2(c3).start()

        c4 = tau - 4

        @when(ok(c4))
        def _():
            c_b2(c4).wait_recv()
            for one in c_load(c4, 0):
                one.wait()

            def put_near(value):
                GS[near_part] = value.astype(BF16)

            def put_far(value):
                GS[far_part] = value.astype(BF16)

            own_part(c4, y, near_part, False, AL, AR, lambda: (A1[c4 % LAND, z],), put_near)
            own_part(c4, y, far_part, True, BL, BR, lambda: (B2[c4 % LAND],), put_far)
            i, layer, at = place(c4)
            here = pl.ds(at, T)
            g = GS[...].astype(F32)
            m = 0.9 * m_out[i, layer, here] + 0.1 * g
            v = 0.95 * v_out[i, layer, here] + 0.05 * g * g
            w = W[c4 % 4].astype(F32)
            out[i, layer, y, z, core, here] = (w - 0.02 * (m * lax.rsqrt(v + 1e-8) + 0.1 * w)).astype(BF16)
            m_out[i, layer, here] = m
            v_out[i, layer, here] = v
            c_yo(c4).start()
            az(c4, z, start)

        for k in (1, 2, 3):
            c = tau - 4 - k
            for b, there in ((z - k, z - k >= 0), (z + k, z + k <= 3)):

                @when(ok(c), there)
                def _():
                    c_az(c, b, True).wait_recv()
                    az(c, b, start)
                    c_ay(c, b).start()

        for k in (0, 1, 2, 3):
            c = tau - 5 - k
            for b, there in ((z - k, z - k >= 0), (z + k, z + k <= 3))[: 1 if k == 0 else 2]:

                @when(ok(c), there)
                def _():
                    if k == 0:
                        c_yo(c).wait_recv()
                    else:
                        c_bz(c, b, True).wait_recv()
                        c_ay(c, b).wait_recv()
                    bz(c, b, start)
                    c_co(c, b).start()

        c10 = tau - 10

        @when(ok(c10))
        def _():
            loop(0, 4, lambda b: c_co(c10, b).wait_recv())

        late = tau - LAG

        @when(ok(late + 2))
        def _():
            sent(c_core(late + 2, 0))

        @when(ok(late))
        def _():
            sent(c_a1(late))

        for go_right in (True, False):
            cb = late - z if go_right else late - 3 + z
            ca = late - 1 - z if go_right else late - 4 + z
            when(ok(cb))(lambda: b1(cb, go_right, sent, False))
            when(ok(ca))(lambda: a2(ca, go_right, sent, False))

        @when(ok(late - 3))
        def _():
            sent(c_b2(late - 3))

        @when(ok(late - 4))
        def _():
            sent(c_yo(late - 4))
            az(late - 4, z, sent)

        for k in (1, 2, 3):
            c = late - 4 - k
            for b, there in ((z - k, z - k >= 0), (z + k, z + k <= 3)):

                @when(ok(c), there)
                def _():
                    az(c, b, sent)
                    sent(c_ay(c, b))

        for k in (0, 1, 2, 3):
            c = late - 5 - k
            for b, there in ((z - k, z - k >= 0), (z + k, z + k <= 3))[: 1 if k == 0 else 2]:

                @when(ok(c), there)
                def _():
                    bz(c, b, sent)
                    sent(c_co(c, b))

    loop(0, N + 2 + 8 + LAG, step)


def whole_step(pieces, near, arrays):
    tiles = arrays[6].shape[1]
    T, N = tiles // pieces, 6 * pieces
    TA, TB = near, T - near
    tile = (16, 128)
    dma = pltpu.SemaphoreType.DMA
    scratch = [
        pltpu.VMEM((RING, 2, 4, T, *tile), BF16),
        pltpu.VMEM((LAND, 2, 4, T, *tile), BF16),
        pltpu.VMEM((LAND, 4, TA, *tile), BF16),
        pltpu.VMEM((LAND, 3, TA, *tile), BF16),
        pltpu.VMEM((LAND, 3, TA, *tile), BF16),
        pltpu.VMEM((LAND, 3, 2, TB, *tile), BF16),
        pltpu.VMEM((LAND, 3, 2, TB, *tile), BF16),
        pltpu.VMEM((LAND, TB, *tile), BF16),
        pltpu.VMEM((4, T, *tile), BF16),
        pltpu.VMEM((T, *tile), BF16),
        dma((RING,)), dma((4, 3)),
        dma((LAND,)), dma((LAND,)), dma((LAND, 3)), dma((LAND, 3)), dma((LAND, 3)), dma((LAND, 3)), dma((LAND,)), dma((LAND,)),
        dma((LAND, 4)), dma((LAND, 4)), dma((LAND, 4)), dma((LAND, 4)),
        dma((RING,)), dma((RING,)), dma((RING, 3)), dma((RING, 3)), dma((RING, 3)), dma((RING, 3)), dma((RING,)), dma((RING,)),
        dma((RING, 4)), dma((RING, 4)), dma((RING, 4)), dma((RING, 4)), dma((RING, 4)), dma((RING, 4)),
    ]

    def body(*refs):
        kernel(pieces, tiles, near, refs[:12], refs[12:15], refs[15:])

    hbm, vmem = (pl.BlockSpec(memory_space=space) for space in (pl.ANY, pltpu.VMEM))
    return pl.pallas_call(
        body,
        out_shape=(
            pltpu.VMEM((3, 2, tiles, *tile), F32),
            pltpu.VMEM((3, 2, tiles, *tile), F32),
            pltpu.VMEM((3, 2, 2, 4, 2, tiles, *tile), BF16),
        ),
        in_specs=[hbm] * 12,
        out_specs=(vmem,) * 3,
        scratch_shapes=scratch,
        compiler_params=pltpu.CompilerParams(collective_id=0, has_side_effects=True, vmem_limit_bytes=VMEM_LIMIT),
    )(*arrays)


def unload(w, m, v):
    def body(*refs):
        given, outs, sems = refs[:3], refs[3:12], refs[12]
        copies = [pltpu.make_async_copy(given[i // 3].at[i % 3], outs[i], sems.at[i]) for i in range(9)]
        for one in copies:
            one.start()
        for one in copies:
            one.wait()

    given = [pltpu.with_memory_space_constraint(a, pltpu.VMEM) for a in (w, m, v)]
    return pl.pallas_call(
        body,
        out_shape=tuple(jax.ShapeDtypeStruct(a.shape[1:], a.dtype) for a in (w, m, v) for _ in range(3)),
        in_specs=[pl.BlockSpec(memory_space=pltpu.VMEM)] * 3,
        out_specs=(pl.BlockSpec(memory_space=pl.ANY),) * 9,
        scratch_shapes=[pltpu.SemaphoreType.DMA((9,))],
        compiler_params=pltpu.CompilerParams(vmem_limit_bytes=1 << 20),
    )(*given)


def to_tiles(a):
    _, r, c = a.shape
    return a.reshape(2, r // 8, 8, c // 128, 128).swapaxes(2, 3).reshape(2, -1, 16, 128)


def from_tiles(a, shape):
    _, r, c = shape
    return a.reshape(2, r // 8, c // 128, 8, 128).swapaxes(2, 3).reshape(shape)


def solution(mesh):
    def step(*arrays):
        arrays = [a.reshape(a.shape[-3:]) for a in arrays]
        tiled = [to_tiles(a) for a in arrays]
        blocks = tiled[6].shape[1]
        tiled = [t.reshape(2, 2, 4, 2, blocks, 16, 128) for t in tiled[:6]] + tiled[6:]
        results = unload(*(lambda r: (r[2], r[0], r[1]))(whole_step(PIECES, 6 * blocks // (10 * PIECES), tiled)))
        shapes = [a.shape for a in arrays[3:9]] + [a.shape for a in arrays[6:9]]
        return tuple(from_tiles(one, shape) for one, shape in zip(results, shapes, strict=True))

    all_of, cut = P(None, None, None), P(None, "dp", None)
    return jax.shard_map(
        step,
        mesh=mesh,
        in_specs=(P(("rep", "dp"), None, None, None),) * 3 + (all_of,) * 3 + (cut,) * 6,
        out_specs=(P("rep", None, None),) * 3 + (P("rep", "dp", None),) * 6,
        check_vma=False,
    )
```

time: 377 us -> 347 us (0.920)
  local copies, waits for them, and re-layouts: 33.1 us -> 0 us
    slice x2 -> x0, local copies, waits for them, and re-layouts: 33.1 us -> none  [the longest x1 26.8 us: step(): w[i]]
    pallas_call x1 -> x2, Pallas kernels: 343 us -> 346 us  [the longest x1 330 us: whole_step(): pl.pallas_call(body, out_shape=(pltpu.VMEM((3, 2, tiles, *tile), F32), pl...]
where the time goes in v2:
time: 347 us
  Pallas kernels  346 us (100%)
    pallas_call x1, Pallas kernels, whole_step(): pl.pallas_call(body, out_shape=(pltpu.VMEM((3, 2, tiles, *tile), F32), pl...  330 us
    pallas_call x1, Pallas kernels, unload(): pl.pallas_call(body, out_shape=tuple((jax.ShapeDtypeStruct(a.shape[1:], a...  15.9 us

profile of v2, /device:TPU:0, one launch (start us, length us, event | category | flops | bytes accessed | tf_op | source)
XLA Modules:
  0.0 346.9 jit_solution(17018142752913502688)
XLA Ops:
  0.6 330.3 %shard_map.187 = (f32[3,2,100,16,128]{4,3,2,1,0:T(8,128)S(1)}, f32[3,2,100,16,128]{4,3,2,1,0:T(8,128)S(1)}, bf16[3,2,2,4,2,100,16,128]{7,6,5,4,3,2,1,0:T(8,128)(2,1)S(1)}) custom-call(bf16[2,2,4,2,100,16,128]{6,5,4,3,2,1,0:T(8,128)(2,1)} %bitcast.105, bf16[2,2,4,2,100,16,128]{6,5,4,3,2,1,0:T(8,128)(2,1)} %bitcast.106, ...), custom_call_target="tpu_custom_call" | custom-call | tf_op jit(solution)/shard_map/pallas_call | solution.py:389
  331.0 15.9 %shard_map.188 = (bf16[2,2,4,2,100,16,128]{6,5,4,3,2,1,0:T(8,128)(2,1)}, bf16[2,2,4,2,100,16,128]{6,5,4,3,2,1,0:T(8,128)(2,1)}, bf16[2,2,4,2,100,16,128]{6,5,4,3...) custom-call(bf16[3,2,2,4,2,100,16,128]{7,6,5,4,3,2,1,0:T(8,128)(2,1), ...), custom_call_target="tpu_custom_call" | custom-call | tf_op jit(solution)/shard_map/pallas_call | solution.py:413

commit v3 on v0

v3 whole, which is shorter than its diff:
```python
import functools

import jax
import jax.numpy as jnp
from jax import lax
from jax.experimental import pallas as pl
from jax.experimental.pallas import tpu as pltpu
from jax.sharding import PartitionSpec as P

PIECES = 10
LAND = 16
RING = 8
LAG = 3
SENDS = 4
VMEM_LIMIT = 15 << 20
F32, BF16 = jnp.float32, jnp.bfloat16


class Chunk:
    def __init__(self, c, count):
        self.c = c
        self.ok = jnp.logical_and(c >= 0, c < count)
        self.s, self.g, self.k = (lax.rem(c + 64, n) for n in (SENDS, RING, LAND))


def kernel(pieces, tiles, near, refs_in, refs_out, scratch):
    g_in, w_in, m_in, v_in = (refs_in[i : i + 3] for i in (0, 3, 6, 9))
    m_out, v_out, out = refs_out
    (G, CL, A1, AL, AR, BL, BR, B2, W, GS) = scratch[:10]
    (l_g, l_mv) = scratch[10:12]
    (r_core, r_a1, r_al, r_ar, r_bl, r_br, r_b2, r_yo, r_az, r_ay, r_bz, r_co) = scratch[12:24]
    (s_core, s_a1, s_al, s_ar, s_bl, s_br, s_b2, s_yo, s_azr, s_azl, s_ay, s_bzr, s_bzl, s_co) = scratch[24:]
    T = tiles // pieces
    TA, TB = near, T - near
    N = 6 * pieces
    x, me = lax.axis_index("rep"), lax.axis_index("dp")
    core, z, y = me % 2, (me // 2) % 4, me // 8
    partner, right, left, across = me + 1 - 2 * core, me + 2, me - 2, me + 8 - 16 * y

    barrier = pltpu.get_barrier_semaphore()

    def greet(device):
        pl.semaphore_signal(barrier, inc=1, device_id=(x, device), device_id_type=pl.DeviceIdType.MESH)

    greet(partner)
    greet(across)

    @pl.when(z > 0)
    def _():
        greet(left)

    @pl.when(z < 3)
    def _():
        greet(right)

    pl.semaphore_wait(barrier, 2 + jnp.where(z > 0, 1, 0) + jnp.where(z < 3, 1, 0))

    def copy(src, dst, ss, rs, device):
        return pltpu.make_async_remote_copy(
            src_ref=src, dst_ref=dst, send_sem=ss, recv_sem=rs, device_id=(x, device), device_id_type=pl.DeviceIdType.MESH
        )

    both, row, near_part, far_part, whole = pl.ds(0, 2), pl.ds(0, 4), pl.ds(0, TA), pl.ds(TA, TB), pl.ds(0, T)

    def place(c):
        layers = lax.div(c, pieces)
        return lax.rem(layers, 2), pl.ds((c - layers * pieces) * T, T)

    def c_core(n, i):
        layer, at = place(n.c)
        return copy(g_in[i].at[layer, both, row, 1 - core, at], CL.at[n.k], s_core.at[n.s], r_core.at[n.g], partner)

    def c_g(n, i):
        layer, at = place(n.c)
        return pltpu.make_async_copy(g_in[i].at[layer, both, row, core, at], G.at[n.g], l_g.at[n.s])

    def c_load(n, i):
        layer, at = place(n.c)
        return (
            pltpu.make_async_copy(m_in[i].at[layer, at], m_out.at[n.c], l_mv.at[n.s, 0]),
            pltpu.make_async_copy(v_in[i].at[layer, at], v_out.at[n.c], l_mv.at[n.s, 1]),
            pltpu.make_async_copy(w_in[i].at[layer, y, z, core, at], W.at[n.s], l_mv.at[n.s, 2]),
        )

    def c_a1(n):
        return copy(CL.at[n.k, 1 - y, row, near_part], A1.at[n.k], s_a1.at[n.s], r_a1.at[n.s], across)

    def c_a2(n, b, go_right):
        land, rs, ss, j, device = (AL, r_al, s_al, b - 1, right) if go_right else (AR, r_ar, s_ar, b, left)
        return copy(CL.at[n.k, y, b, near_part], land.at[n.k, j], ss.at[n.s, j], rs.at[n.s, j], device)

    def c_b1(n, b, go_right):
        land, rs, ss, j, device = (BL, r_bl, s_bl, b - 1, right) if go_right else (BR, r_br, s_br, b, left)
        return copy(CL.at[n.k, both, b, far_part], land.at[n.k, j], ss.at[n.s, j], rs.at[n.s, j], device)

    def c_b2(n):
        return copy(CL.at[n.k, 1 - y, z, far_part], B2.at[n.k], s_b2.at[n.s], r_b2.at[n.s], across)

    def same(n, rows, column, part, ss, rs, device):
        there = out.at[n.c, rows, column, core, part]
        return copy(there, there, ss, rs, device)

    def c_yo(n):
        return same(n, y, z, whole, s_yo.at[n.s], r_yo.at[n.s], across)

    def c_az(n, b, go_right):
        ss, device = (s_azr, right) if go_right else (s_azl, left)
        return same(n, y, b, near_part, ss.at[n.s, b], r_az.at[n.s, b], device)

    def c_ay(n, b):
        return same(n, y, b, near_part, s_ay.at[n.s, b], r_ay.at[n.s, b], across)

    def c_bz(n, b, go_right):
        ss, device = (s_bzr, right) if go_right else (s_bzl, left)
        return same(n, both, b, far_part, ss.at[n.s, b], r_bz.at[n.s, b], device)

    def c_co(n, b):
        return same(n, both, b, whole, s_co.at[n.s, b], r_co.at[n.k], partner)

    def c_co_all(n):
        return same(n, both, row, whole, s_co.at[n.s, 0], r_co.at[n.k], partner)

    def start(copies):
        for one in copies if isinstance(copies, tuple) else (copies,):
            one.start()

    def sent(one):
        one.wait_send()

    def when(*conds):
        return pl.when(functools.reduce(jnp.logical_and, conds))

    def loop(low, high, body):
        lax.fori_loop(low, high, lambda i, _: (body(i), 0)[1], 0)

    def of_weight(n, do):
        for i in range(3):
            when(n.c >= 2 * i * pieces, n.c < 2 * (i + 1) * pieces)(functools.partial(do, i))

    def total(terms):
        return functools.reduce(jnp.add, (one.astype(F32) for one in terms))

    def a2(n, go_right, act, sums):
        def one(b):
            if sums:

                def put(inner):
                    terms = [G[n.g, y, b, near_part], CL[n.k, y, b, near_part], A1[n.k, b]]
                    if inner:
                        terms.append(AL[n.k, b - 1] if go_right else AR[n.k, b])
                    CL[n.k, y, b, near_part] = total(terms).astype(BF16)

                pl.when(z == (0 if go_right else 3))(lambda: put(False))
                pl.when(z != (0 if go_right else 3))(lambda: put(True))
            act(c_a2(n, b, go_right))

        loop(z + 1, 4, one) if go_right else loop(0, z, one)

    def b1(n, go_right, act, sums):
        def one(b):
            if sums:

                def put(inner):
                    terms = [G[n.g, both, b, far_part], CL[n.k, both, b, far_part]]
                    if inner:
                        terms.append(BL[n.k, b - 1] if go_right else BR[n.k, b])
                    CL[n.k, both, b, far_part] = total(terms).astype(BF16)

                pl.when(z == (0 if go_right else 3))(lambda: put(False))
                pl.when(z != (0 if go_right else 3))(lambda: put(True))
            act(c_b1(n, b, go_right))

        loop(z + 1, 4, one) if go_right else loop(0, z, one)

    def arrived(n, go_right, make):
        if go_right:
            when(z > 0)(lambda: loop(z, 4, lambda b: make(n, b, True).wait_recv()))
        else:
            when(z < 3)(lambda: loop(0, z + 1, lambda b: make(n, b, False).wait_recv()))

    def own_part(n, yy, part, with_rows, land_l, land_r, extra, put):
        def terms():
            return [G[n.g, yy, z, part], CL[n.k, yy, z, part], *extra()]

        def from_left():
            return land_l[n.k, z - 1, yy] if with_rows else land_l[n.k, z - 1]

        def from_right():
            return land_r[n.k, z, yy] if with_rows else land_r[n.k, z]

        pl.when(z == 0)(lambda: put(total([*terms(), from_right()])))
        pl.when(z == 3)(lambda: put(total([*terms(), from_left()])))
        when(z > 0, z < 3)(lambda: put(total([*terms(), from_left(), from_right()])))

    def az(n, b, act):
        when(z < 3, b <= z)(lambda: act(c_az(n, b, True)))
        when(z > 0, b >= z)(lambda: act(c_az(n, b, False)))

    def bz(n, b, act):
        when(z < 3, b <= z)(lambda: act(c_bz(n, b, True)))
        when(z > 0, b >= z)(lambda: act(c_bz(n, b, False)))

    def sides(k):
        return ((z, z >= 0),) if k == 0 else ((z - k, z >= k), (z + k, z <= 3 - k))

    def step(t):
        tau = t - 2
        back = [Chunk(tau - k, N) for k in range(9 + LAG)]
        inward = {
            (late, kind, go_right): Chunk(tau - late - kind - (z if go_right else 3 - z), N)
            for late in (0, LAG)
            for kind in (0, 1)
            for go_right in (True, False)
        }
        first, ahead, last = Chunk(t, N), Chunk(t - 4, N), Chunk(tau - 10, N)

        @pl.when(first.ok)
        def _():
            of_weight(first, lambda i: (start(c_core(first, i)), start(c_g(first, i)), None)[2])

        @pl.when(ahead.ok)
        def _():
            of_weight(ahead, lambda i: start(c_load(ahead, i)))

        n0 = back[0]

        @pl.when(n0.ok)
        def _():
            c_g(n0, 0).wait()
            c_core(n0, 0).wait_recv()
            CL[n0.k, 1 - y, row, near_part] = total((G[n0.g, 1 - y, row, near_part], CL[n0.k, 1 - y, row, near_part])).astype(BF16)
            c_a1(n0).start()

        for go_right in (True, False):
            n = inward[0, 0, go_right]

            @pl.when(n.ok)
            def _():
                arrived(n, go_right, c_b1)
                b1(n, go_right, start, True)

        @pl.when(back[1].ok)
        def _():
            c_a1(back[1]).wait_recv()

        for go_right in (True, False):
            n = inward[0, 1, go_right]

            @pl.when(n.ok)
            def _():
                arrived(n, go_right, c_a2)
                a2(n, go_right, start, True)

        n3 = back[3]

        @pl.when(n3.ok)
        def _():
            def put(value):
                CL[n3.k, 1 - y, z, far_part] = value.astype(BF16)

            own_part(n3, 1 - y, far_part, True, BL, BR, lambda: (), put)
            c_b2(n3).start()

        n4 = back[4]

        @pl.when(n4.ok)
        def _():
            c_b2(n4).wait_recv()
            for one in c_load(n4, 0):
                one.wait()

            def put_near(value):
                GS[near_part] = value.astype(BF16)

            def put_far(value):
                GS[far_part] = value.astype(BF16)

            own_part(n4, y, near_part, False, AL, AR, lambda: (A1[n4.k, z],), put_near)
            own_part(n4, y, far_part, True, BL, BR, lambda: (B2[n4.k],), put_far)
            g = GS[...].astype(F32)
            m = 0.9 * m_out[n4.c] + 0.1 * g
            v = 0.95 * v_out[n4.c] + 0.05 * g * g
            w = W[n4.s].astype(F32)
            out[n4.c, y, z, core] = (w - 0.02 * (m * lax.rsqrt(v + 1e-8) + 0.1 * w)).astype(BF16)
            m_out[n4.c] = m
            v_out[n4.c] = v
            c_yo(n4).start()
            az(n4, z, start)

        for k in (1, 2, 3):
            n = back[4 + k]
            for b, there in sides(k):

                @when(n.ok, there)
                def _():
                    c_az(n, b, True).wait_recv()
                    az(n, b, start)
                    c_ay(n, b).start()

        for k in (0, 1, 2, 3):
            n = back[5 + k]
            for b, there in sides(k):

                @when(n.ok, there)
                def _():
                    if k == 0:
                        c_yo(n).wait_recv()
                    else:
                        c_bz(n, b, True).wait_recv()
                        c_ay(n, b).wait_recv()
                    bz(n, b, start)
                    c_co(n, b).start()

        @pl.when(last.ok)
        def _():
            c_co_all(last).wait_recv()

        @pl.when(back[LAG].ok)
        def _():
            sent(c_core(back[LAG], 0))
            sent(c_a1(back[LAG]))

        for go_right in (True, False):
            for kind, group in enumerate((b1, a2)):
                n = inward[LAG, kind, go_right]
                pl.when(n.ok)(functools.partial(group, n, go_right, sent, False))

        @pl.when(back[LAG + 3].ok)
        def _():
            sent(c_b2(back[LAG + 3]))

        @pl.when(back[LAG + 4].ok)
        def _():
            sent(c_yo(back[LAG + 4]))
            az(back[LAG + 4], z, sent)

        for k in (1, 2, 3):
            n = back[LAG + 4 + k]
            for b, there in sides(k):

                @when(n.ok, there)
                def _():
                    az(n, b, sent)
                    sent(c_ay(n, b))

        for k in (0, 1, 2, 3):
            n = back[LAG + 5 + k]
            for b, there in sides(k):

                @when(n.ok, there)
                def _():
                    bz(n, b, sent)
                    sent(c_co(n, b))

    loop(0, N + 2 + 8 + LAG, step)


def whole_step(pieces, near, arrays):
    tiles = arrays[6].shape[1]
    T, N = tiles // pieces, 6 * pieces
    TA, TB = near, T - near
    tile = (16, 128)
    dma = pltpu.SemaphoreType.DMA
    scratch = [
        pltpu.VMEM((RING, 2, 4, T, *tile), BF16),
        pltpu.VMEM((LAND, 2, 4, T, *tile), BF16),
        pltpu.VMEM((LAND, 4, TA, *tile), BF16),
        pltpu.VMEM((LAND, 3, TA, *tile), BF16),
        pltpu.VMEM((LAND, 3, TA, *tile), BF16),
        pltpu.VMEM((LAND, 3, 2, TB, *tile), BF16),
        pltpu.VMEM((LAND, 3, 2, TB, *tile), BF16),
        pltpu.VMEM((LAND, TB, *tile), BF16),
        pltpu.VMEM((SENDS, T, *tile), BF16),
        pltpu.VMEM((T, *tile), BF16),
        dma((SENDS,)), dma((SENDS, 3)),
        dma((RING,)), dma((SENDS,)), dma((SENDS, 3)), dma((SENDS, 3)), dma((SENDS, 3)), dma((SENDS, 3)), dma((SENDS,)), dma((SENDS,)),
        dma((SENDS, 4)), dma((SENDS, 4)), dma((SENDS, 4)), dma((LAND,)),
        dma((SENDS,)), dma((SENDS,)), dma((SENDS, 3)), dma((SENDS, 3)), dma((SENDS, 3)), dma((SENDS, 3)), dma((SENDS,)), dma((SENDS,)),
        dma((SENDS, 4)), dma((SENDS, 4)), dma((SENDS, 4)), dma((SENDS, 4)), dma((SENDS, 4)), dma((SENDS, 4)),
    ]

    def body(*refs):
        kernel(pieces, tiles, near, refs[:12], refs[12:15], refs[15:])

    hbm, vmem = (pl.BlockSpec(memory_space=space) for space in (pl.ANY, pltpu.VMEM))
    return pl.pallas_call(
        body,
        out_shape=(
            pltpu.VMEM((N, T, *tile), F32),
            pltpu.VMEM((N, T, *tile), F32),
            pltpu.VMEM((N, 2, 4, 2, T, *tile), BF16),
        ),
        in_specs=[hbm] * 12,
        out_specs=(vmem,) * 3,
        scratch_shapes=scratch,
        compiler_params=pltpu.CompilerParams(collective_id=0, has_side_effects=True, vmem_limit_bytes=VMEM_LIMIT),
    )(*arrays)


def unload(m, v, w):
    N, T, *tile = m.shape
    pieces = N // 6

    def body(m, v, w, *refs):
        outs, sems = refs[:9], refs[9]
        every = [pl.ds(0, n) for n in (2, 4, 2)]
        for i in range(3):
            for c in range(2 * pieces):
                there = outs[i].at[(c // pieces, *every, c % pieces)]
                pltpu.make_async_copy(w.at[2 * i * pieces + c], there, sems.at[i]).start()
            here = pl.ds(2 * i * pieces, 2 * pieces)
            pltpu.make_async_copy(m.at[here], outs[3 + i], sems.at[3 + i]).start()
            pltpu.make_async_copy(v.at[here], outs[6 + i], sems.at[6 + i]).start()
        for i in range(9):
            pltpu.make_async_copy(outs[i], outs[i], sems.at[i]).wait()

    given = [pltpu.with_memory_space_constraint(a, pltpu.VMEM) for a in (m, v, w)]
    return pl.pallas_call(
        body,
        out_shape=(jax.ShapeDtypeStruct((2, 2, 4, 2, pieces, T, *tile), BF16),) * 3
        + (jax.ShapeDtypeStruct((2 * pieces, T, *tile), F32),) * 6,
        in_specs=[pl.BlockSpec(memory_space=pltpu.VMEM)] * 3,
        out_specs=(pl.BlockSpec(memory_space=pl.ANY),) * 9,
        scratch_shapes=[pltpu.SemaphoreType.DMA((9,))],
        compiler_params=pltpu.CompilerParams(vmem_limit_bytes=1 << 20),
    )(*given)


def to_tiles(a):
    _, r, c = a.shape
    return a.reshape(2, r // 8, 8, c // 128, 128).swapaxes(2, 3).reshape(2, -1, 16, 128)


def from_tiles(a, shape):
    _, r, c = shape
    return a.reshape(2, r // 8, c // 128, 8, 128).swapaxes(2, 3).reshape(shape)


def solution(mesh):
    def step(*arrays):
        arrays = [a.reshape(a.shape[-3:]) for a in arrays]
        tiled = [to_tiles(a) for a in arrays]
        blocks = tiled[6].shape[1]
        tiled = [t.reshape(2, 2, 4, 2, blocks, 16, 128) for t in tiled[:6]] + tiled[6:]
        results = unload(*whole_step(PIECES, 6 * blocks // (10 * PIECES), tiled))
        shapes = [a.shape for a in arrays[3:9]] + [a.shape for a in arrays[6:9]]
        return tuple(from_tiles(one, shape) for one, shape in zip(results, shapes, strict=True))

    all_of, cut = P(None, None, None), P(None, "dp", None)
    return jax.shard_map(
        step,
        mesh=mesh,
        in_specs=(P(("rep", "dp"), None, None, None),) * 3 + (all_of,) * 3 + (cut,) * 6,
        out_specs=(P("rep", None, None),) * 3 + (P("rep", "dp", None),) * 6,
        check_vma=False,
    )
```

time: 782 us -> 342 us (0.44)
  waiting for transfers between devices: 696 us -> 0 us
  Pallas kernels: 0 us -> 341 us
  local copies, waits for them, and re-layouts: 58.8 us -> 0 us
  between operations: 14.2 us -> 0.65 us
  other arithmetic: 12.8 us -> 0 us
    pallas_call x0 -> x2, Pallas kernels: none -> 341 us  [the longest x1 325 us: whole_step(): pl.pallas_call(body, out_shape=(pltpu.VMEM((N, T, *tile), F32), pltpu.VME...]
    all_gather x3 -> x0, waiting for transfers between devices: 308 us -> none  [step(): whole = [lax.all_gather(one[0], 'dp', axis=1, tiled=True) for one in new]]
    reduce_scatter x2 -> x0, waiting for transfers between devices: 250 us -> none  [step(): lax.psum_scatter(t[0], 'dp', scatter_dimension=1, tiled=True)]
    unnamed x7 -> x0, waiting for transfers between devices: 138 us -> none
    unnamed x22 -> x0, local copies, waits for them, and re-layouts: 58.8 us -> none
    convert_element_type x3 -> x0, other arithmetic: 12.8 us -> none  [adamw(): return ((w - 0.02 * step).astype(jnp.bfloat16), m, v)]
  transfers between devices with their start and end apart: 6 -> 0, of which waited for: 6 -> 0; matrix products, arithmetic and copies ran while one was open for 6% -> 0% of each run, Pallas kernels for 0% -> 0%
where the time goes in v3:
time: 342 us
  Pallas kernels  341 us (100%)
    pallas_call x1, Pallas kernels, whole_step(): pl.pallas_call(body, out_shape=(pltpu.VMEM((N, T, *tile), F32), pltpu.VME...  325 us
    pallas_call x1, Pallas kernels, unload(): pl.pallas_call(body, out_shape=(jax.ShapeDtypeStruct((2, 2, 4, 2, pieces,...  15.7 us

profile of v3, /device:TPU:0, one launch (start us, length us, event | category | flops | bytes accessed | tf_op | source)
XLA Modules:
  0.0 341.7 jit_solution(4842319397180696984)
XLA Ops:
  0.6 325.4 %shard_map.187 = (f32[60,10,16,128]{3,2,1,0:T(8,128)S(1)}, f32[60,10,16,128]{3,2,1,0:T(8,128)S(1)}, bf16[60,2,4,2,10,16,128]{6,5,4,3,2,1,0:T(8,128)(2,1)S(1)}) custom-call(bf16[2,2,4,2,100,16,128]{6,5,4,3,2,1,0:T(8,128)(2,1)} %bitcast.105, bf16[2,2,4,2,100,16,128]{6,5,4,3,2,1,0:T(8,128)(2,1)} %bitcast.106, bf16[2,2,4,2,100,16,128]{6,5,4,3,2,1,0:T(8,128)(2,1)} %bitcast.107, ...), custom_call_target="tpu_custom_call" | custom-call | tf_op jit(solution)/shard_map/pallas_call | solution.py:386
  326.0 15.7 %shard_map.188 = (bf16[2,2,4,2,10,10,16,128]{7,6,5,4,3,2,1,0:T(8,128)(2,1)}, bf16[2,2,4,2,10,10,16,128]{7,6,5,4,3,2,1,0:T(8,128)(2,1)}, bf16[2,2,4,2,10,10,16,12...) custom-call(f32[60,10,16,128]{3,2,1,0:T(8,128)S(1)} %get-tuple-eleme, ...), custom_call_target="tpu_custom_call" | custom-call | tf_op jit(solution)/shard_map/pallas_call | solution.py:418

commit v4 on v3

--- a/solution.py
+++ b/solution.py
@@ -1,4 +1,5 @@
 import functools
+import itertools
 
 import jax
 import jax.numpy as jnp
@@ -10,8 +11,9 @@
 PIECES = 10
 LAND = 16
 RING = 8
-LAG = 3
-SENDS = 4
+LAG = 1
+SENDS = 2
+ARRIVALS = 4
 VMEM_LIMIT = 15 << 20
 F32, BF16 = jnp.float32, jnp.bfloat16
 
@@ -20,7 +22,7 @@
     def __init__(self, c, count):
         self.c = c
         self.ok = jnp.logical_and(c >= 0, c < count)
-        self.s, self.g, self.k = (lax.rem(c + 64, n) for n in (SENDS, RING, LAND))
+        self.s, self.r, self.g, self.k = (lax.rem(c + 64, n) for n in (SENDS, ARRIVALS, RING, LAND))
 
 
 def kernel(pieces, tiles, near, refs_in, refs_out, scratch):
@@ -35,7 +37,8 @@
     N = 6 * pieces
     x, me = lax.axis_index("rep"), lax.axis_index("dp")
     core, z, y = me % 2, (me // 2) % 4, me // 8
-    partner, right, left, across = me + 1 - 2 * core, me + 2, me - 2, me + 8 - 16 * y
+    plane, other = (core + y + z) % 2, 1 - 2 * core
+    partner, right, left, across = me + other, me + 2 + other, me - 2 + other, me + 8 - 16 * y + other
 
     barrier = pltpu.get_barrier_semaphore()
 
@@ -66,53 +69,67 @@
         layers = lax.div(c, pieces)
         return lax.rem(layers, 2), pl.ds((c - layers * pieces) * T, T)
 
+    def at_z(b):
+        return 2 * lax.rem(b, 2) + lax.div(b, 2)
+
+    def terms_of(n, i, which, slot):
+        layer, at = place(n.c)
+        for yy in range(2):
+            for odd in range(2):
+                its = which if yy == odd else 1 - which
+                yield g_in[i].at[layer, yy, both, odd, its, at], slot.at[yy, pl.ds(2 * odd, 2)]
+
     def c_core(n, i):
-        layer, at = place(n.c)
-        return copy(g_in[i].at[layer, both, row, 1 - core, at], CL.at[n.k], s_core.at[n.s], r_core.at[n.g], partner)
+        return tuple(copy(src, dst, s_core.at[n.r], r_core.at[n.g], partner) for src, dst in terms_of(n, i, 1 - plane, CL.at[n.k]))
+
+    def c_core_all(n):
+        return copy(CL.at[n.k], CL.at[n.k], s_core.at[n.r], r_core.at[n.g], partner)
 
     def c_g(n, i):
-        layer, at = place(n.c)
-        return pltpu.make_async_copy(g_in[i].at[layer, both, row, core, at], G.at[n.g], l_g.at[n.s])
+        return tuple(pltpu.make_async_copy(src, dst, l_g.at[n.r]) for src, dst in terms_of(n, i, plane, G.at[n.g]))
+
+    def c_g_all(n):
+        return pltpu.make_async_copy(G.at[n.g], G.at[n.g], l_g.at[n.r])
 
     def c_load(n, i):
         layer, at = place(n.c)
         return (
-            pltpu.make_async_copy(m_in[i].at[layer, at], m_out.at[n.c], l_mv.at[n.s, 0]),
-            pltpu.make_async_copy(v_in[i].at[layer, at], v_out.at[n.c], l_mv.at[n.s, 1]),
-            pltpu.make_async_copy(w_in[i].at[layer, y, z, core, at], W.at[n.s], l_mv.at[n.s, 2]),
+            pltpu.make_async_copy(m_in[i].at[layer, at], m_out.at[n.c], l_mv.at[n.r, 0]),
+            pltpu.make_async_copy(v_in[i].at[layer, at], v_out.at[n.c], l_mv.at[n.r, 1]),
+            pltpu.make_async_copy(w_in[i].at[layer, y, z, core, at], W.at[n.r], l_mv.at[n.r, 2]),
         )
 
     def c_a1(n):
-        return copy(CL.at[n.k, 1 - y, row, near_part], A1.at[n.k], s_a1.at[n.s], r_a1.at[n.s], across)
+        return copy(CL.at[n.k, 1 - y, row, near_part], A1.at[n.k], s_a1.at[n.s], r_a1.at[n.r], across)
 
     def c_a2(n, b, go_right):
         land, rs, ss, j, device = (AL, r_al, s_al, b - 1, right) if go_right else (AR, r_ar, s_ar, b, left)
-        return copy(CL.at[n.k, y, b, near_part], land.at[n.k, j], ss.at[n.s, j], rs.at[n.s, j], device)
+        return copy(CL.at[n.k, y, at_z(b), near_part], land.at[n.k, j], ss.at[n.s, j], rs.at[n.r, j], device)
 
     def c_b1(n, b, go_right):
         land, rs, ss, j, device = (BL, r_bl, s_bl, b - 1, right) if go_right else (BR, r_br, s_br, b, left)
-        return copy(CL.at[n.k, both, b, far_part], land.at[n.k, j], ss.at[n.s, j], rs.at[n.s, j], device)
+        return copy(CL.at[n.k, both, at_z(b), far_part], land.at[n.k, j], ss.at[n.s, j], rs.at[n.r, j], device)
 
     def c_b2(n):
-        return copy(CL.at[n.k, 1 - y, z, far_part], B2.at[n.k], s_b2.at[n.s], r_b2.at[n.s], across)
+        return copy(CL.at[n.k, 1 - y, at_z(z), far_part], B2.at[n.k], s_b2.at[n.s], r_b2.at[n.r], across)
 
     def same(n, rows, column, part, ss, rs, device):
-        there = out.at[n.c, rows, column, core, part]
+        there = out.at[n.c, rows, column, plane, part]
         return copy(there, there, ss, rs, device)
 
     def c_yo(n):
-        return same(n, y, z, whole, s_yo.at[n.s], r_yo.at[n.s], across)
+        return same(n, y, z, whole, s_yo.at[n.s], r_yo.at[n.r], across)
 
     def c_az(n, b, go_right):
         ss, device = (s_azr, right) if go_right else (s_azl, left)
-        return same(n, y, b, near_part, ss.at[n.s, b], r_az.at[n.s, b], device)
+        return same(n, y, b, near_part, ss.at[n.s, b], r_az.at[n.r, b], device)
 
     def c_ay(n, b):
-        return same(n, y, b, near_part, s_ay.at[n.s, b], r_ay.at[n.s, b], across)
+        return same(n, y, b, near_part, s_ay.at[n.s, b], r_ay.at[n.r, b], across)
 
     def c_bz(n, b, go_right):
         ss, device = (s_bzr, right) if go_right else (s_bzl, left)
-        return same(n, both, b, far_part, ss.at[n.s, b], r_bz.at[n.s, b], device)
+        return same(n, both, b, far_part, ss.at[n.s, b], r_bz.at[n.r, b], device)
 
     def c_co(n, b):
         return same(n, both, b, whole, s_co.at[n.s, b], r_co.at[n.k], partner)
@@ -145,10 +162,11 @@
             if sums:
 
                 def put(inner):
-                    terms = [G[n.g, y, b, near_part], CL[n.k, y, b, near_part], A1[n.k, b]]
+                    spot = at_z(b)
+                    terms = [G[n.g, y, spot, near_part], CL[n.k, y, spot, near_part], A1[n.k, spot]]
                     if inner:
                         terms.append(AL[n.k, b - 1] if go_right else AR[n.k, b])
-                    CL[n.k, y, b, near_part] = total(terms).astype(BF16)
+                    CL[n.k, y, spot, near_part] = total(terms).astype(BF16)
 
                 pl.when(z == (0 if go_right else 3))(lambda: put(False))
                 pl.when(z != (0 if go_right else 3))(lambda: put(True))
@@ -161,10 +179,11 @@
             if sums:
 
                 def put(inner):
-                    terms = [G[n.g, both, b, far_part], CL[n.k, both, b, far_part]]
+                    spot = at_z(b)
+                    terms = [G[n.g, both, spot, far_part], CL[n.k, both, spot, far_part]]
                     if inner:
                         terms.append(BL[n.k, b - 1] if go_right else BR[n.k, b])
-                    CL[n.k, both, b, far_part] = total(terms).astype(BF16)
+                    CL[n.k, both, spot, far_part] = total(terms).astype(BF16)
 
                 pl.when(z == (0 if go_right else 3))(lambda: put(False))
                 pl.when(z != (0 if go_right else 3))(lambda: put(True))
@@ -180,7 +199,7 @@
 
     def own_part(n, yy, part, with_rows, land_l, land_r, extra, put):
         def terms():
-            return [G[n.g, yy, z, part], CL[n.k, yy, z, part], *extra()]
+            return [G[n.g, yy, at_z(z), part], CL[n.k, yy, at_z(z), part], *extra()]
 
         def from_left():
             return land_l[n.k, z - 1, yy] if with_rows else land_l[n.k, z - 1]
@@ -212,7 +231,7 @@
             for kind in (0, 1)
             for go_right in (True, False)
         }
-        first, ahead, last = Chunk(t, N), Chunk(t - 4, N), Chunk(tau - 10, N)
+        first, ahead, last = Chunk(t, N), Chunk(t - 4, N), Chunk(tau - 9, N)
 
         @pl.when(first.ok)
         def _():
@@ -226,8 +245,8 @@
 
         @pl.when(n0.ok)
         def _():
-            c_g(n0, 0).wait()
-            c_core(n0, 0).wait_recv()
+            c_g_all(n0).wait()
+            c_core_all(n0).wait_recv()
             CL[n0.k, 1 - y, row, near_part] = total((G[n0.g, 1 - y, row, near_part], CL[n0.k, 1 - y, row, near_part])).astype(BF16)
             c_a1(n0).start()
 
@@ -256,7 +275,7 @@
         @pl.when(n3.ok)
         def _():
             def put(value):
-                CL[n3.k, 1 - y, z, far_part] = value.astype(BF16)
+                CL[n3.k, 1 - y, at_z(z), far_part] = value.astype(BF16)
 
             own_part(n3, 1 - y, far_part, True, BL, BR, lambda: (), put)
             c_b2(n3).start()
@@ -275,13 +294,13 @@
             def put_far(value):
                 GS[far_part] = value.astype(BF16)
 
-            own_part(n4, y, near_part, False, AL, AR, lambda: (A1[n4.k, z],), put_near)
+            own_part(n4, y, near_part, False, AL, AR, lambda: (A1[n4.k, at_z(z)],), put_near)
             own_part(n4, y, far_part, True, BL, BR, lambda: (B2[n4.k],), put_far)
             g = GS[...].astype(F32)
             m = 0.9 * m_out[n4.c] + 0.1 * g
             v = 0.95 * v_out[n4.c] + 0.05 * g * g
-            w = W[n4.s].astype(F32)
-            out[n4.c, y, z, core] = (w - 0.02 * (m * lax.rsqrt(v + 1e-8) + 0.1 * w)).astype(BF16)
+            w = W[n4.r].astype(F32)
+            out[n4.c, y, z, plane] = (w - 0.02 * (m * lax.rsqrt(v + 1e-8) + 0.1 * w)).astype(BF16)
             m_out[n4.c] = m
             v_out[n4.c] = v
             c_yo(n4).start()
@@ -317,7 +336,7 @@
 
         @pl.when(back[LAG].ok)
         def _():
-            sent(c_core(back[LAG], 0))
+            sent(c_core_all(back[LAG]))
             sent(c_a1(back[LAG]))
 
         for go_right in (True, False):
@@ -370,13 +389,13 @@
         pltpu.VMEM((LAND, 3, 2, TB, *tile), BF16),
         pltpu.VMEM((LAND, 3, 2, TB, *tile), BF16),
         pltpu.VMEM((LAND, TB, *tile), BF16),
-        pltpu.VMEM((SENDS, T, *tile), BF16),
+        pltpu.VMEM((ARRIVALS, T, *tile), BF16),
         pltpu.VMEM((T, *tile), BF16),
-        dma((SENDS,)), dma((SENDS, 3)),
-        dma((RING,)), dma((SENDS,)), dma((SENDS, 3)), dma((SENDS, 3)), dma((SENDS, 3)), dma((SENDS, 3)), dma((SENDS,)), dma((SENDS,)),
-        dma((SENDS, 4)), dma((SENDS, 4)), dma((SENDS, 4)), dma((LAND,)),
-        dma((SENDS,)), dma((SENDS,)), dma((SENDS, 3)), dma((SENDS, 3)), dma((SENDS, 3)), dma((SENDS, 3)), dma((SENDS,)), dma((SENDS,)),
-        dma((SENDS, 4)), dma((SENDS, 4)), dma((SENDS, 4)), dma((SENDS, 4)), dma((SENDS, 4)), dma((SENDS, 4)),
+        dma((ARRIVALS,)), dma((ARRIVALS, 3)),
+        dma((RING,)), dma((ARRIVALS,)), *(dma((ARRIVALS, 3)) for _ in range(4)), dma((ARRIVALS,)), dma((ARRIVALS,)),
+        *(dma((ARRIVALS, 4)) for _ in range(3)), dma((LAND,)),
+        dma((ARRIVALS,)), dma((SENDS,)), *(dma((SENDS, 3)) for _ in range(4)), dma((SENDS,)), dma((SENDS,)),
+        *(dma((SENDS, 4)) for _ in range(6)),
     ]
 
     def body(*refs):
@@ -403,11 +422,17 @@
 
     def body(m, v, w, *refs):
         outs, sems = refs[:9], refs[9]
-        every = [pl.ds(0, n) for n in (2, 4, 2)]
         for i in range(3):
-            for c in range(2 * pieces):
-                there = outs[i].at[(c // pieces, *every, c % pieces)]
-                pltpu.make_async_copy(w.at[2 * i * pieces + c], there, sems.at[i]).start()
+
+            def one(c, _, i=i):
+                layer = lax.div(c, pieces)
+                for y, z in itertools.product(range(2), range(4)):
+                    for plane in range(2):
+                        there = outs[i].at[layer, y, z, (plane + y + z) % 2, c - layer * pieces]
+                        pltpu.make_async_copy(w.at[2 * i * pieces + c, y, z, plane], there, sems.at[i]).start()
+                return 0
+
+            lax.fori_loop(0, 2 * pieces, one, 0)
             here = pl.ds(2 * i * pieces, 2 * pieces)
             pltpu.make_async_copy(m.at[here], outs[3 + i], sems.at[3 + i]).start()
             pltpu.make_async_copy(v.at[here], outs[6 + i], sems.at[6 + i]).start()
@@ -441,7 +466,7 @@
         arrays = [a.reshape(a.shape[-3:]) for a in arrays]
         tiled = [to_tiles(a) for a in arrays]
         blocks = tiled[6].shape[1]
-        tiled = [t.reshape(2, 2, 4, 2, blocks, 16, 128) for t in tiled[:6]] + tiled[6:]
+        tiled = [t.reshape(2, 2, 2, 2, 2, blocks, 16, 128) for t in tiled[:3]] + [t.reshape(2, 2, 4, 2, blocks, 16, 128) for t in tiled[3:6]] + tiled[6:]
         results = unload(*whole_step(PIECES, 6 * blocks // (10 * PIECES), tiled))
         shapes = [a.shape for a in arrays[3:9]] + [a.shape for a in arrays[6:9]]
         return tuple(from_tiles(one, shape) for one, shape in zip(results, shapes, strict=True))

time: 342 us -> 338 us (0.988)
  Pallas kernels: 341 us -> 337 us
where the time goes in v4:
time: 338 us
  Pallas kernels  337 us (100%)
    pallas_call x1, Pallas kernels, whole_step(): pl.pallas_call(body, out_shape=(pltpu.VMEM((N, T, *tile), F32), pltpu.VME...  322 us
    pallas_call x1, Pallas kernels, unload(): pl.pallas_call(body, out_shape=(jax.ShapeDtypeStruct((2, 2, 4, 2, pieces,...  15.4 us

profile of v4, /device:TPU:0, one launch (start us, length us, event | category | flops | bytes accessed | tf_op | source)
XLA Modules:
  0.0 338.1 jit_solution(14300919691990464024)
XLA Ops:
  0.6 322.0 %shard_map.187 = (f32[60,10,16,128]{3,2,1,0:T(8,128)S(1)}, f32[60,10,16,128]{3,2,1,0:T(8,128)S(1)}, bf16[60,2,4,2,10,16,128]{6,5,4,3,2,1,0:T(8,128)(2,1)S(1)}) custom-call(bf16[2,2,2,2,2,100,16,128]{7,6,5,4,3,2,1,0:T(8,128)(2,1)} %bitcast.105, bf16[2,2,2,2,2,100,16,128]{7,6,5,4,3,2,1,0:T(8,128)(2,1)} %bitcast.106, ...), custom_call_target="tpu_custom_call" | custom-call | tf_op jit(solution)/shard_map/pallas_call | solution.py:405
  322.6 15.4 %shard_map.188 = (bf16[2,2,4,2,10,10,16,128]{7,6,5,4,3,2,1,0:T(8,128)(2,1)}, bf16[2,2,4,2,10,10,16,128]{7,6,5,4,3,2,1,0:T(8,128)(2,1)}, bf16[2,2,4,2,10,10,16,12...) custom-call(f32[60,10,16,128]{3,2,1,0:T(8,128)S(1)} %get-tuple-eleme, ...), custom_call_target="tpu_custom_call" | custom-call | tf_op jit(solution)/shard_map/pallas_call | solution.py:443

commit v5 on v4

--- a/solution.py
+++ b/solution.py
@@ -428,14 +428,14 @@
                 layer = lax.div(c, pieces)
                 for y, z in itertools.product(range(2), range(4)):
                     for plane in range(2):
-                        there = outs[i].at[layer, y, z, (plane + y + z) % 2, c - layer * pieces]
-                        pltpu.make_async_copy(w.at[2 * i * pieces + c, y, z, plane], there, sems.at[i]).start()
+                        for part in (pl.ds(0, T // 2), pl.ds(T // 2, T - T // 2)):
+                            there = outs[i].at[layer, y, z, (plane + y + z) % 2, c - layer * pieces, part]
+                            pltpu.make_async_copy(w.at[2 * i * pieces + c, y, z, plane, part], there, sems.at[i]).start()
+                for given, j in ((m, 3 + i), (v, 6 + i)):
+                    pltpu.make_async_copy(given.at[2 * i * pieces + c], outs[j].at[c], sems.at[j]).start()
                 return 0
 
             lax.fori_loop(0, 2 * pieces, one, 0)
-            here = pl.ds(2 * i * pieces, 2 * pieces)
-            pltpu.make_async_copy(m.at[here], outs[3 + i], sems.at[3 + i]).start()
-            pltpu.make_async_copy(v.at[here], outs[6 + i], sems.at[6 + i]).start()
         for i in range(9):
             pltpu.make_async_copy(outs[i], outs[i], sems.at[i]).wait()
 

time: 338 us -> 338 us (level)
  no operation moved by 1% of the time
where the time goes in v5:
time: 338 us; the launch traced here: 337 us
  Pallas kernels  337 us (100%)
    pallas_call x1, Pallas kernels, whole_step(): pl.pallas_call(body, out_shape=(pltpu.VMEM((N, T, *tile), F32), pltpu.VME...  322 us
    pallas_call x1, Pallas kernels, unload(): pl.pallas_call(body, out_shape=(jax.ShapeDtypeStruct((2, 2, 4, 2, pieces,...  14.8 us

profile of v5, /device:TPU:0, one launch (start us, length us, event | category | flops | bytes accessed | tf_op | source)
XLA Modules:
  0.0 337.5 jit_solution(11939974864895476014)
XLA Ops:
  0.6 322.0 %shard_map.187 = (f32[60,10,16,128]{3,2,1,0:T(8,128)S(1)}, f32[60,10,16,128]{3,2,1,0:T(8,128)S(1)}, bf16[60,2,4,2,10,16,128]{6,5,4,3,2,1,0:T(8,128)(2,1)S(1)}) custom-call(bf16[2,2,2,2,2,100,16,128]{7,6,5,4,3,2,1,0:T(8,128)(2,1)} %bitcast.105, bf16[2,2,2,2,2,100,16,128]{7,6,5,4,3,2,1,0:T(8,128)(2,1)} %bitcast.106, ...), custom_call_target="tpu_custom_call" | custom-call | tf_op jit(solution)/shard_map/pallas_call | solution.py:405
  322.6 14.8 %shard_map.188 = (bf16[2,2,4,2,10,10,16,128]{7,6,5,4,3,2,1,0:T(8,128)(2,1)}, bf16[2,2,4,2,10,10,16,128]{7,6,5,4,3,2,1,0:T(8,128)(2,1)}, bf16[2,2,4,2,10,10,16,12...) custom-call(f32[60,10,16,128]{3,2,1,0:T(8,128)S(1)} %get-tuple-eleme, ...), custom_call_target="tpu_custom_call" | custom-call | tf_op jit(solution)/shard_map/pallas_call | solution.py:443
